TPU v7x, 32 devices: a whole 2x2x4 slice. The times are simulated.
32 devices in a mesh: group: 2 (over y), ha: 4 (over x, core), wa: 4 (over z).
Axes of the slice: x: 2, y: 2, z: 4, core: 2. Of those that a mesh axis runs over, the one named last changes fastest.
Arguments:
- queries: bfloat16 [4, 32, 32, 1536], P('group', 'ha', 'wa'), parts along dimension 0, may hold values from -6 to 6
- keys: bfloat16 [4, 32, 32, 1536], P('group', 'ha', 'wa'), parts along dimension 0, may hold values from -6 to 6
- values: bfloat16 [4, 32, 32, 1536], P('group', 'ha', 'wa'), parts along dimension 0, may hold values from -6 to 6
- out_grad: bfloat16 [4, 32, 32, 1536], P('group', 'ha', 'wa'), parts along dimension 0, may hold values from -96 to 96
- log_norm: float32 [12, 4, 32, 32], P(None, 'group', 'ha', 'wa'), parts along dimension 1, may hold values from 6.5 to 7.5
- delta_rows: float32 [12, 4, 32, 32], P(None, 'group', 'ha', 'wa'), parts along dimension 1, may hold values from -360 to 360
- text_keys: bfloat16 [64, 1536], P('group'), parts along dimension 0, may hold values from -6 to 6
- text_values: bfloat16 [64, 1536], P('group'), parts along dimension 0, may hold values from -6 to 6
- window_table: int32 [4, 4, 9], replicated, may hold values 0 or 1
Outputs:
- query_grad: bfloat16 [4, 32, 32, 1536], P('group', 'ha', 'wa'), parts along dimension 0
- key_grad: bfloat16 [4, 32, 32, 1536], P('group', 'ha', 'wa'), parts along dimension 0
- value_grad: bfloat16 [4, 32, 32, 1536], P('group', 'ha', 'wa'), parts along dimension 0
- text_key_grad: bfloat16 [64, 1536], P('group'), parts along dimension 0
- text_value_grad: bfloat16 [64, 1536], P('group'), parts along dimension 0
There are 2 independent parts, one for each index of `group`. A program takes and returns all parts, laid end to end along the dimension named above; an argument that names none is the same for every part. Nothing has to cross between parts.
All inputs are finite; a program needn't handle non-finite values.
Results may differ from a plain program's by a relative error of at most 0.001.
The roundings to bfloat16 on the way count: a program that leaves them out, or rounds other values in their place, can miss the bound.
Values may be sent and summed in bfloat16 or wider, within the bound.
A program may use at most 64 MiB of HBM per device.

v0:
```python
import math
import jax
import jax.numpy as jnp
from jax import lax
from jax.sharding import PartitionSpec as P

HEADS = 12
HDIM = 128
TILE = 8
HALO = 2


def passed_along(value, axis, steps):
    count = lax.axis_size(axis)
    pairs = [(source, (source + steps) % count) for source in range(count)]
    return lax.ppermute(value, axis, pairs)


def with_halo(cells, sides, width):
    for axis, dim in sides:
        count = lax.axis_size(axis)
        head = lax.slice_in_dim(cells, 0, width, axis=dim)
        tail = lax.slice_in_dim(cells, cells.shape[dim] - width, cells.shape[dim], axis=dim)
        cells = jnp.concatenate(
            [
                lax.ppermute(tail, axis, [(i, (i + 1) % count) for i in range(count)]),
                cells,
                lax.ppermute(head, axis, [((i + 1) % count, i) for i in range(count)]),
            ],
            axis=dim,
        )
    return cells


def tile_grads(query_rows, cotangent_rows, norm_rows, delta_part, key_rows, value_rows, cell_mask):
    score_scale = 1.0 / math.sqrt(query_rows.shape[-1])
    scores = (
        jnp.einsum("qhd,khd->hqk", query_rows, key_rows, preferred_element_type=jnp.float32)
        * score_scale
    )
    probs = jnp.exp(scores - norm_rows[:, :, None])
    if cell_mask is not None:
        probs = probs * cell_mask[None, None, :]
    probs_half = probs.astype(jnp.bfloat16)
    value_part = jnp.einsum(
        "hqk,qhd->khd", probs_half, cotangent_rows, preferred_element_type=jnp.float32
    )
    prob_grad = jnp.einsum(
        "qhd,khd->hqk", cotangent_rows, value_rows, preferred_element_type=jnp.float32
    )
    score_grad = (probs * (prob_grad - delta_part[:, :, None])).astype(jnp.bfloat16)
    query_part = (
        jnp.einsum("hqk,khd->qhd", score_grad, key_rows, preferred_element_type=jnp.float32)
        * score_scale
    )
    key_part = (
        jnp.einsum("hqk,qhd->khd", score_grad, query_rows, preferred_element_type=jnp.float32)
        * score_scale
    )
    return (query_part, key_part, value_part)


def send_cols(strip, offset):
    return passed_along(strip, "wa", offset)


def send_rows(strip, offset):
    return passed_along(strip, "ha", offset)


def fold_band(buffer, along, mover):
    lower = lax.slice_in_dim(buffer, 0, HALO, axis=along)
    middle = lax.slice_in_dim(buffer, HALO, HALO + TILE, axis=along)
    upper = lax.slice_in_dim(buffer, HALO + TILE, TILE + 2 * HALO, axis=along)
    from_before = mover(upper, 1)
    from_after = mover(lower, -1)
    widths_low = [(0, 0)] * buffer.ndim
    widths_high = [(0, 0)] * buffer.ndim
    widths_low[along] = (0, TILE - HALO)
    widths_high[along] = (TILE - HALO, 0)
    return middle + jnp.pad(from_before, widths_low) + jnp.pad(from_after, widths_high)


def local(
    queries, keys, values, out_grad, log_norm, delta_rows, text_keys, text_values, window_table
):
    frames, tile_side, _, width = queries.shape
    window_side = TILE + 2 * HALO
    stacked = jnp.stack((keys, values))
    window = with_halo(stacked, (("ha", 2), ("wa", 3)), HALO)
    row_tile = lax.axis_index("ha")
    col_tile = lax.axis_index("wa")
    anchor = jnp.zeros((), jnp.int32)
    pattern = (
        lax.dynamic_slice(window_table, (row_tile, col_tile, anchor), (1, 1, 9))
        .reshape(3, 3)
        .astype(jnp.float32)
    )
    position = jnp.arange(window_side, dtype=jnp.int32)
    block_of = (position >= HALO).astype(jnp.int32) + (position >= HALO + TILE).astype(jnp.int32)
    one_hot = (block_of[:, None] == jnp.arange(3, dtype=jnp.int32)[None, :]).astype(jnp.float32)
    cell_grid = jnp.dot(
        jnp.dot(one_hot, pattern, precision=lax.Precision.HIGHEST),
        one_hot.T,
        precision=lax.Precision.HIGHEST,
    )
    cell_mask = jnp.broadcast_to(cell_grid[None], (frames, window_side, window_side)).reshape(-1)
    query_rows = queries.reshape(-1, HEADS, HDIM)
    cotangent_rows = out_grad.reshape(-1, HEADS, HDIM)
    norm_rows = log_norm.reshape(HEADS, -1)
    delta_part = delta_rows.reshape(HEADS, -1)
    key_rows = window[0].reshape(-1, HEADS, HDIM)
    value_rows = window[1].reshape(-1, HEADS, HDIM)
    video_query, video_key, video_value = tile_grads(
        query_rows, cotangent_rows, norm_rows, delta_part, key_rows, value_rows, cell_mask
    )
    text_query, text_key, text_value = tile_grads(
        query_rows,
        cotangent_rows,
        norm_rows,
        delta_part,
        text_keys.reshape(-1, HEADS, HDIM),
        text_values.reshape(-1, HEADS, HDIM),
        None,
    )
    query_grad = (
        (video_query + text_query).astype(jnp.bfloat16).reshape(frames, tile_side, tile_side, width)
    )
    text_total = lax.psum(jnp.stack((text_key, text_value)), ("ha", "wa"))
    buffer = jnp.stack((video_key, video_value)).reshape(2, frames, window_side, window_side, width)
    buffer = fold_band(buffer, 2, send_rows)
    buffer = fold_band(buffer, 3, send_cols)
    text_key_grad = text_total[0].reshape(-1, width).astype(jnp.bfloat16)
    text_value_grad = text_total[1].reshape(-1, width).astype(jnp.bfloat16)
    return (
        query_grad,
        buffer[0].astype(jnp.bfloat16),
        buffer[1].astype(jnp.bfloat16),
        text_key_grad,
        text_value_grad,
    )


def solution(mesh):
    in_specs = (
        P("group", "ha", "wa", None),
        P("group", "ha", "wa", None),
        P("group", "ha", "wa", None),
        P("group", "ha", "wa", None),
        P(None, "group", "ha", "wa"),
        P(None, "group", "ha", "wa"),
        P("group", None),
        P("group", None),
        P(),
    )
    out_specs = (
        P("group", "ha", "wa", None),
        P("group", "ha", "wa", None),
        P("group", "ha", "wa", None),
        P("group", None),
        P("group", None),
    )
    return jax.shard_map(local, mesh=mesh, in_specs=in_specs, out_specs=out_specs, check_vma=False)
```

profile of v0, /device:TPU:0, one launch (start us, length us, event | category | flops | bytes accessed | tf_op | source)
XLA Modules:
  0.0 151.5 jit_solution(18392472798687320180)
XLA Ops:
  0.6 0.0 copy-start
  0.7 1.1 pad_maximum_fusion.7
  1.8 0.5 collective-permute-start
  2.4 2.0 %collective-permute-start.1 = (bf16[2,2,2,8,1536]{4,3,2,1,0:T(8,128)(2,1)S(1)}, bf16[2,2,2,8,1536]{4,3,2,1,0:T(8,128)(2,1)S(1)}, u32[]{:S(2)}, u32[]{:S(2)}) collective-permute-start(bf16[2,2,2,8,1536]{4,3,2,1,0:T(8,128)(2,1)S(1)} %get-tuple-element.21), channel_id=1, source_target_pairs={{4,0},{8,4},{12,8},{0,12},{5,1},{9,5},{13,9},{1,13},{6,2},{10,6},{... | collective-permute-start | bytes 589832 | tf_op jit(solution)/shard_map/ppermute | solution.py:28
  4.3 0.7 convert_reduce_fusion
  5.0 0.1 convert_element_type.67
  5.1 0.2 fusion.32
  5.3 0.2 fusion.31
  5.5 0.9 copy.59
  6.4 0.9 copy.62
  7.4 1.4 reshape.49
  8.8 0.3 reshape.50
  9.0 0.3 fusion.10
  9.4 0.3 fusion.11
  9.7 0.7 copy-done.9
  10.4 0.2 fusion.7
  10.6 0.1 mul.62
  10.7 0.2 convolution_bitcast_fusion.1
  10.9 0.0 collective-permute-done
  10.9 0.0 collective-permute-done.1
  10.9 0.0 copy-done.7
  11.0 1.2 pad_maximum_fusion.5
  12.1 2.3 %collective-permute-start.2 = (bf16[2,2,12,2,1536]{4,3,2,1,0:T(2,128)(2,1)}, bf16[2,2,12,2,1536]{4,3,2,1,0:T(2,128)(2,1)S(1)}, u32[]{:S(2)}, u32[]{:S(2)}) collective-permute-start(bf16[2,2,12,2,1536]{4,3,2,1,0:T(2,128)(2,1)} %get-tuple-element.16), channel_id=1, source_target_pairs={{0,1},{1,2},{2,3},{3,0},{4,5},{5,6},{6,7},{7,4},{8,9},{9,10},{10,1... | collective-permute-start | bytes 884744 | tf_op jit(solution)/shard_map/ppermute | solution.py:26
  14.5 2.0 %collective-permute-start.3 = (bf16[2,2,12,2,1536]{4,3,2,1,0:T(2,128)(2,1)}, bf16[2,2,12,2,1536]{4,3,2,1,0:T(2,128)(2,1)S(1)}, u32[]{:S(2)}, u32[]{:S(2)}) collective-permute-start(bf16[2,2,12,2,1536]{4,3,2,1,0:T(2,128)(2,1)} %get-tuple-element.17), channel_id=1, source_target_pairs={{1,0},{2,1},{3,2},{0,3},{5,4},{6,5},{7,6},{4,7},{9,8},{10,9},{11,1... | collective-permute-start | bytes 884744 | tf_op jit(solution)/shard_map/ppermute | solution.py:28
  16.5 73.5 %all-reduce.5 = bf16[2,32,12,128]{3,1,2,0:T(8,128)(2,1)} all-reduce(f32[2,32,12,128]{3,1,2,0:T(8,128)S(1)} %pad_maximum_fusion.1), channel_id=1, replica_groups=mesh['group'=2,'ha'=4,'wa'=4] {'ha','wa'}, use_global_device_ids=true, to_apply=%region_0.0 | all-reduce | flops 98304 | bytes 589824 | tf_op jit(solution)/shard_map/psum | solution.py:129
  90.0 0.0 collective-permute-done.2
  90.0 1.5 pad_maximum_fusion
  91.5 0.2 fusion.38
  91.7 1.7 %reshape_squeeze.9 = bf16[288,12,128]{2,1,0:T(8,128)(2,1)} reshape(bf16[1,2,12,12,1536]{4,3,2,1,0:T(8,128)(2,1)S(1)} %get-tuple-element.14) | data formatting | bytes 1769472 | tf_op jit(solution)/shard_map/reshape;squeeze | solution.py:113
  93.3 0.8 reshape_squeeze.8
  94.2 0.6 exponential_multiply_fusion
  94.7 1.6 %convolution_bitcast_fusion = f32[288,12,128]{2,0,1:T(8,128)} fusion(f32[12,288,128]{2,1,0:T(8,128)S(1)} %exponential_multiply_fusion, bf16[128,12,128]{2,1,0:T(8,128)(2,1)S(1)} %reshape.50), kind=kOutput, calls=%fused_computation.9 | convolution fusion | flops 113688576 | bytes 3932160 | tf_op jit(solution)/shard_map/hqk,qhd->khd/dot_general | solution.py:45
  96.4 0.5 multiply_convert_fusion
  96.9 0.4 multiply_bitcast_fusion
  97.2 0.5 copy-done.2
  97.8 2.5 %copy.75 = f32[288,12,128]{2,1,0:T(8,128)} copy(f32[288,12,128]{2,0,1:T(8,128)S(1)} %multiply_bitcast_fusion) | data formatting | bytes 3538944 | tf_op jit(solution)/shard_map/mul | solution.py:57
  100.3 2.4 %stack.30 = f32[1,2,12,12,1536]{4,3,2,1,0:T(8,128)S(1)} reshape(f32[288,12,128]{2,1,0:T(8,128)} %copy.75) | data formatting | bytes 3538944 | tf_op jit(solution)/shard_map/stack | solution.py:130
  102.7 4.0 %copy.77 = f32[288,12,128]{2,1,0:T(8,128)} copy(f32[288,12,128]{2,0,1:T(8,128)} %convolution_bitcast_fusion) | data formatting | bytes 3538944 | tf_op jit(solution)/shard_map/hqk,qhd->khd/transpose | solution.py:45
  106.6 3.2 %stack.31 = f32[1,2,12,12,1536]{4,3,2,1,0:T(8,128)} reshape(f32[288,12,128]{2,1,0:T(8,128)} %copy.77) | data formatting | bytes 3538944 | tf_op jit(solution)/shard_map/stack | solution.py:130
  109.8 0.2 constant_dynamic-update-slice_fusion.1
  110.1 1.4 copy-done.1
  111.5 0.2 constant_dynamic-update-slice_fusion
  111.7 0.0 copy-start.11
  111.8 0.1 fusion.36
  111.9 0.5 copy.78
  112.4 0.5 copy.80
  112.8 0.1 collective-permute-start.5
  112.9 0.5 collective-permute-start.4
  113.5 0.7 copy_bitcast_fusion
  114.2 12.1 %collective-permute-done.5 = f32[2,2,2,12,1536]{4,2,3,1,0:T(2,128)S(1)} collective-permute-done((f32[2,2,2,12,1536]{4,2,3,1,0:T(2,128)S(1)}, f32[2,2,2,12,1536]{4,2,3,1,0:T(2,128)S(1)}, u32[]{:S(2)}, u32[]{:S(2)}) %collective-permute-start.5) | collective-permute-done | bytes 589856 | tf_op jit(solution)/shard_map/ppermute | solution.py:16
  126.3 0.1 copy.81
  126.4 1.4 collective-permute-done.4
  127.9 0.1 copy.79
  128.0 0.4 fusion
  128.4 1.2 fusion.37
  129.6 3.8 %collective-permute-start.7 = (f32[2,2,8,2,1536]{4,3,2,1,0:T(2,128)}, f32[2,2,8,2,1536]{4,3,2,1,0:T(2,128)}, u32[]{:S(2)}, u32[]{:S(2)}) collective-permute-start(f32[2,2,8,2,1536]{4,3,2,1,0:T(2,128)} %get-tuple-element.13), channel_id=1, source_target_pairs={{0,3},{1,0},{2,1},{3,2},{4,7},{5,4},{6,5},{7,6},{8,11},{9,8},{10,9... | collective-permute-start | bytes 1179656 | tf_op jit(solution)/shard_map/ppermute | solution.py:16
  133.5 0.6 fusion.5
  134.1 1.1 fusion.6
  135.1 2.2 %copy.73 = bf16[128,12,128]{2,1,0:T(8,128)(2,1)} copy(bf16[128,12,128]{0,2,1:T(8,128)(2,1)} %fusion.6) | data formatting | bytes 786432 | tf_op jit(solution)/shard_map/convert_element_type | solution.py:127
  137.3 2.1 %reshape.53 = bf16[2,8,8,1536]{3,2,1,0:T(8,128)(2,1)} reshape(bf16[128,12,128]{2,1,0:T(8,128)(2,1)} %copy.73) | data formatting | bytes 786432 | tf_op jit(solution)/shard_map/reshape | solution.py:127
  139.4 4.4 %collective-permute-done.6 = f32[2,2,8,2,1536]{4,3,2,1,0:T(2,128)} collective-permute-done((f32[2,2,8,2,1536]{4,3,2,1,0:T(2,128)}, f32[2,2,8,2,1536]{4,3,2,1,0:T(2,128)}, u32[]{:S(2)}, u32[]{:S(2)}) %collective-permute-start.6) | collective-permute-done | bytes 393248 | tf_op jit(solution)/shard_map/ppermute | solution.py:16
  143.7 5.2 %collective-permute-done.7 = f32[2,2,8,2,1536]{4,3,2,1,0:T(2,128)} collective-permute-done((f32[2,2,8,2,1536]{4,3,2,1,0:T(2,128)}, f32[2,2,8,2,1536]{4,3,2,1,0:T(2,128)}, u32[]{:S(2)}, u32[]{:S(2)}) %collective-permute-start.7) | collective-permute-done | bytes 393248 | tf_op jit(solution)/shard_map/ppermute | solution.py:16
  149.0 1.6 %fusion.2 = bf16[2,2,8,8,1536]{4,3,2,1,0:T(8,128)(2,1)S(1)} fusion(f32[2,2,8,12,1536]{4,3,2,1,0:T(8,128)S(1)} %fusion, f32[2,2,8,2,1536]{4,3,2,1,0:T(2,128)} %collective-permute-done.7, f32[2,2,8,2,1536]{4,3,2,1,0:T(2,128)} %collective-permute-done.6), kind=kLoop, calls=%fused_computation.8 | loop fusion | flops 1179648 | bytes 3145728 | tf_op jit(solution)/shard_map/convert.3
  150.5 0.9 slice_bitcast_fusion
  (30 shorter events, 0.2 us)
Async XLA Ops:
  0.6 8.4 %copy-start = (bf16[32,1536]{1,0:T(8,128)(2,1)S(1)}, bf16[32,1536]{1,0:T(8,128)(2,1)}, u32[]{:S(2)}) copy-start(bf16[32,1536]{1,0:T(8,128)(2,1)} %param.15) | copy-start | bytes 294916
  0.6 8.1 %copy-start.12 = (bf16[2,8,8,1536]{3,2,1,0:T(8,128)(2,1)S(1)}, bf16[2,8,8,1536]{3,2,1,0:T(8,128)(2,1)}, u32[]{:S(2)}) copy-start(bf16[2,8,8,1536]{3,2,1,0:T(8,128)(2,1)} %param.12) | copy-start | bytes 1179652
  0.7 8.7 %copy-start.13 = (bf16[32,1536]{1,0:T(8,128)(2,1)S(1)}, bf16[32,1536]{1,0:T(8,128)(2,1)}, u32[]{:S(2)}) copy-start(bf16[32,1536]{1,0:T(8,128)(2,1)} %param.16) | copy-start | bytes 294916
  1.8 9.1 %collective-permute-start = (bf16[2,2,2,8,1536]{4,3,2,1,0:T(8,128)(2,1)S(1)}, bf16[2,2,2,8,1536]{4,3,2,1,0:T(8,128)(2,1)S(1)}, u32[]{:S(2)}, u32[]{:S(2)}) collective-permute-start(bf16[2,2,2,8,1536]{4,3,2,1,0:T(8,128)(2,1)S(1)} %get-tuple-element.20), channel_id=1, source_target_pairs={{0,4},{4,8},{8,12},{12,0},{1,5},{5,9},{9,13},{13,1},{2,6},{6,10},{... | collective-permute-start | bytes 589832 | tf_op jit(solution)/shard_map/ppermute | solution.py:26
  2.4 8.6 %collective-permute-start.1 = (bf16[2,2,2,8,1536]{4,3,2,1,0:T(8,128)(2,1)S(1)}, bf16[2,2,2,8,1536]{4,3,2,1,0:T(8,128)(2,1)S(1)}, u32[]{:S(2)}, u32[]{:S(2)}) collective-permute-start(bf16[2,2,2,8,1536]{4,3,2,1,0:T(8,128)(2,1)S(1)} %get-tuple-element.21), channel_id=1, source_target_pairs={{4,0},{8,4},{12,8},{0,12},{5,1},{9,5},{13,9},{1,13},{6,2},{10,6},{... | collective-permute-start | bytes 589832 | tf_op jit(solution)/shard_map/ppermute | solution.py:28
  7.4 3.6 %copy-start.7 = (bf16[2,8,8,1536]{3,2,1,0:T(8,128)(2,1)S(1)}, bf16[2,8,8,1536]{3,2,1,0:T(8,128)(2,1)}, u32[]{:S(2)}) copy-start(bf16[2,8,8,1536]{3,2,1,0:T(8,128)(2,1)} %param.11) | copy-start | bytes 1179652
  7.4 3.6 %copy-start.8 = (bf16[2,8,8,1536]{3,2,1,0:T(8,128)(2,1)S(1)}, bf16[2,8,8,1536]{3,2,1,0:T(8,128)(2,1)}, u32[]{:S(2)}) copy-start(bf16[2,8,8,1536]{3,2,1,0:T(8,128)(2,1)} %param.10) | copy-start | bytes 1179652
  9.7 0.7 copy-start.9
  12.1 77.9 %collective-permute-start.2 = (bf16[2,2,12,2,1536]{4,3,2,1,0:T(2,128)(2,1)}, bf16[2,2,12,2,1536]{4,3,2,1,0:T(2,128)(2,1)S(1)}, u32[]{:S(2)}, u32[]{:S(2)}) collective-permute-start(bf16[2,2,12,2,1536]{4,3,2,1,0:T(2,128)(2,1)} %get-tuple-element.16), channel_id=1, source_target_pairs={{0,1},{1,2},{2,3},{3,0},{4,5},{5,6},{6,7},{7,4},{8,9},{9,10},{10,1... | collective-permute-start | bytes 884744 | tf_op jit(solution)/shard_map/ppermute | solution.py:26
  14.5 75.5 %collective-permute-start.3 = (bf16[2,2,12,2,1536]{4,3,2,1,0:T(2,128)(2,1)}, bf16[2,2,12,2,1536]{4,3,2,1,0:T(2,128)(2,1)S(1)}, u32[]{:S(2)}, u32[]{:S(2)}) collective-permute-start(bf16[2,2,12,2,1536]{4,3,2,1,0:T(2,128)(2,1)} %get-tuple-element.17), channel_id=1, source_target_pairs={{1,0},{2,1},{3,2},{0,3},{5,4},{6,5},{7,6},{4,7},{9,8},{10,9},{11,1... | collective-permute-start | bytes 884744 | tf_op jit(solution)/shard_map/ppermute | solution.py:28
  94.1 2.2 %copy-start.4 = (bf16[288,12,128]{2,1,0:T(8,128)(2,1)}, bf16[288,12,128]{2,1,0:T(8,128)(2,1)S(1)}, u32[]{:S(2)}) copy-start(bf16[288,12,128]{2,1,0:T(8,128)(2,1)S(1)} %reshape_squeeze.8) | copy-start | bytes 2654212
  94.7 1.6 %copy-start.6 = (bf16[288,12,128]{2,1,0:T(8,128)(2,1)S(1)}, bf16[288,12,128]{2,1,0:T(8,128)(2,1)}, u32[]{:S(2)}) copy-start(bf16[288,12,128]{2,1,0:T(8,128)(2,1)} %reshape_squeeze.9) | copy-start | bytes 2654212
  96.8 0.9 copy-start.2
  109.8 1.7 %copy-start.1 = (f32[1,2,12,12,1536]{4,3,2,1,0:T(8,128)S(1)}, f32[1,2,12,12,1536]{4,3,2,1,0:T(8,128)}, u32[]{:S(2)}) copy-start(f32[1,2,12,12,1536]{4,3,2,1,0:T(8,128)} %stack.31) | copy-start | bytes 5308420
  111.7 1.6 %copy-start.11 = (bf16[2,32,12,128]{3,1,2,0:T(8,128)(2,1)S(1)}, bf16[2,32,12,128]{3,1,2,0:T(8,128)(2,1)}, u32[]{:S(2)}) copy-start(bf16[2,32,12,128]{3,1,2,0:T(8,128)(2,1)} %all-reduce.5) | copy-start | bytes 589828
  112.8 13.5 %collective-permute-start.5 = (f32[2,2,2,12,1536]{4,2,3,1,0:T(2,128)S(1)}, f32[2,2,2,12,1536]{4,2,3,1,0:T(2,128)S(1)}, u32[]{:S(2)}, u32[]{:S(2)}) collective-permute-start(f32[2,2,2,12,1536]{4,2,3,1,0:T(2,128)S(1)} %copy.80), channel_id=1, source_target_pairs={{0,12},{4,0},{8,4},{12,8},{1,13},{5,1},{9,5},{13,9},{2,14},{6,2},{... | collective-permute-start | bytes 1769480 | tf_op jit(solution)/shard_map/ppermute | solution.py:16
  112.9 15.0 %collective-permute-start.4 = (f32[2,2,2,12,1536]{4,2,3,1,0:T(2,128)S(1)}, f32[2,2,2,12,1536]{4,2,3,1,0:T(2,128)S(1)}, u32[]{:S(2)}, u32[]{:S(2)}) collective-permute-start(f32[2,2,2,12,1536]{4,2,3,1,0:T(2,128)S(1)} %copy.78), channel_id=1, source_target_pairs={{0,4},{4,8},{8,12},{12,0},{1,5},{5,9},{9,13},{13,1},{2,6},{6,10},{... | collective-permute-start | bytes 1769480 | tf_op jit(solution)/shard_map/ppermute | solution.py:16
  128.0 5.5 %copy-start.3 = (bf16[12,288,128]{2,1,0:T(8,128)(2,1)S(1)}, bf16[12,288,128]{2,1,0:T(8,128)(2,1)}, u32[]{:S(2)}) copy-start(bf16[12,288,128]{2,1,0:T(8,128)(2,1)} %copy-done.2) | copy-start | bytes 2654212
  128.0 5.4 %copy-start.5 = (bf16[288,12,128]{2,1,0:T(8,128)(2,1)S(1)}, bf16[288,12,128]{2,1,0:T(8,128)(2,1)}, u32[]{:S(2)}) copy-start(bf16[288,12,128]{2,1,0:T(8,128)(2,1)} %copy-done.4) | copy-start | bytes 2654212
  128.4 5.6 %copy-start.10 = (bf16[12,128,32]{1,2,0:T(8,128)(2,1)S(1)}, bf16[12,128,32]{1,2,0:T(8,128)(2,1)}, u32[]{:S(2)}) copy-start(bf16[12,128,32]{1,2,0:T(8,128)(2,1)} %copy-done.9) | copy-start | bytes 294916
  129.6 14.1 %collective-permute-start.6 = (f32[2,2,8,2,1536]{4,3,2,1,0:T(2,128)}, f32[2,2,8,2,1536]{4,3,2,1,0:T(2,128)}, u32[]{:S(2)}, u32[]{:S(2)}) collective-permute-start(f32[2,2,8,2,1536]{4,3,2,1,0:T(2,128)} %get-tuple-element.12), channel_id=1, source_target_pairs={{0,1},{1,2},{2,3},{3,0},{4,5},{5,6},{6,7},{7,4},{8,9},{9,10},{10,1... | collective-permute-start | bytes 1179656 | tf_op jit(solution)/shard_map/ppermute | solution.py:16
  129.6 19.3 %collective-permute-start.7 = (f32[2,2,8,2,1536]{4,3,2,1,0:T(2,128)}, f32[2,2,8,2,1536]{4,3,2,1,0:T(2,128)}, u32[]{:S(2)}, u32[]{:S(2)}) collective-permute-start(f32[2,2,8,2,1536]{4,3,2,1,0:T(2,128)} %get-tuple-element.13), channel_id=1, source_target_pairs={{0,3},{1,0},{2,1},{3,2},{4,7},{5,4},{6,5},{7,6},{8,11},{9,8},{10,9... | collective-permute-start | bytes 1179656 | tf_op jit(solution)/shard_map/ppermute | solution.py:16
where the time goes:
time: 152 us; the launch traced here: 151 us
  blocking collectives  73.5 us (48%)
  local copies, waits for them, and re-layouts  30 us (20%)
  waiting for transfers between devices  23.1 us (15%)
  starting transfers between devices  11.3 us (7%)
  other arithmetic  6.52 us (4%)
  matrix products  6.17 us (4%)
    psum x1, blocking collectives, local(): text_total = lax.psum(jnp.stack((text_key, text_value)), ('ha', 'wa'))  73.5 us
    ppermute x4, waiting for transfers between devices, passed_along(): return lax.ppermute(value, axis, pairs)  23.1 us
    another operation x3, local copies, waits for them, and re-layouts, local(): jnp.stack((video_key, video_value))  5.81 us
    ppermute x4, starting transfers between devices, passed_along(): return lax.ppermute(value, axis, pairs)  4.38 us
    ppermute x2, starting transfers between devices, with_halo(): lax.ppermute(head, axis, [((i + 1) % count, i) for i in range(count)])  4.01 us
    transpose x1, local copies, waits for them, and re-layouts, tile_grads(): jnp.einsum('hqk,qhd->khd', probs_half, cotangent_rows, preferred_element_...  3.98 us
  transfers between devices with their start and end apart: 8, of which 4 were waited for; matrix products, arithmetic and copies ran while one was open for 8% of the time, Pallas kernels for 0%

commit v1 on v0

--- a/solution.py
+++ b/solution.py
@@ -126,7 +126,7 @@
     query_grad = (
         (video_query + text_query).astype(jnp.bfloat16).reshape(frames, tile_side, tile_side, width)
     )
-    text_total = lax.psum(jnp.stack((text_key, text_value)), ("ha", "wa"))
+    text_total = jnp.sum(lax.all_gather(jnp.stack((text_key, text_value)), ("ha", "wa")), axis=0)
     buffer = jnp.stack((video_key, video_value)).reshape(2, frames, window_side, window_side, width)
     buffer = fold_band(buffer, 2, send_rows)
     buffer = fold_band(buffer, 3, send_cols)

time: 152 us -> 127 us (0.84)
  blocking collectives: 73.5 us -> 0 us
  waiting for transfers between devices: 23.1 us -> 55.2 us
  between operations: 0.96 us -> 14.4 us
  other arithmetic: 6.52 us -> 9.58 us
    psum x1 -> x0, blocking collectives: 73.5 us -> none  [local(): text_total = lax.psum(jnp.stack((text_key, text_value)), ('ha', 'wa'))]
    ppermute x2, waiting for transfers between devices: 0.01 us -> 15.1 us  [with_halo(): lax.ppermute(tail, axis, [(i, (i + 1) % count) for i in range(count)])]
    ppermute x2, waiting for transfers between devices: 0.01 us -> 14.6 us  [with_halo(): lax.ppermute(head, axis, [((i + 1) % count, i) for i in range(count)])]
    reduce_sum x0 -> x1, other arithmetic: none -> 3.51 us  [local(): jnp.sum(lax.all_gather(jnp.stack((text_key, text_value)), ('ha', 'wa')),...]
    ppermute x4, waiting for transfers between devices: 23.1 us -> 25.5 us  [passed_along(): return lax.ppermute(value, axis, pairs)]
    unnamed x29 -> x27, local copies, waits for them, and re-layouts: 2.91 us -> 3.47 us
  transfers between devices with their start and end apart: 8 -> 9, of which waited for: 4 -> 8; matrix products, arithmetic and copies ran while one was open for 8% -> 25% of each run, Pallas kernels for 0% -> 0%
where the time goes in v1:
time: 127 us
  waiting for transfers between devices  55.2 us (43%)
  local copies, waits for them, and re-layouts  30.2 us (24%)
  between operations  14.4 us (11%)
  starting transfers between devices  10.8 us (9%)
  other arithmetic  9.58 us (8%)
  matrix products  6.46 us (5%)
    ppermute x4, waiting for transfers between devices, passed_along(): return lax.ppermute(value, axis, pairs)  25.5 us
    ppermute x2, waiting for transfers between devices, with_halo(): lax.ppermute(tail, axis, [(i, (i + 1) % count) for i in range(count)])  15.1 us
    ppermute x2, waiting for transfers between devices, with_halo(): lax.ppermute(head, axis, [((i + 1) % count, i) for i in range(count)])  14.6 us
    another operation x3, local copies, waits for them, and re-layouts, local(): jnp.stack((video_key, video_value))  5.83 us
    ppermute x4, starting transfers between devices, passed_along(): return lax.ppermute(value, axis, pairs)  4.42 us
    ppermute x2, starting transfers between devices, with_halo(): lax.ppermute(head, axis, [((i + 1) % count, i) for i in range(count)])  4.23 us
    reduce_sum x1, other arithmetic, local(): jnp.sum(lax.all_gather(jnp.stack((text_key, text_value)), ('ha', 'wa')),...  3.51 us
    unnamed x27, local copies, waits for them, and re-layouts  3.47 us
  transfers between devices with their start and end apart: 9, of which 8 were waited for; matrix products, arithmetic and copies ran while one was open for 25% of the time, Pallas kernels for 0%

profile of v1, /device:TPU:0, one launch (start us, length us, event | category | flops | bytes accessed | tf_op | source)
XLA Modules:
  0.0 126.6 jit_solution(12010934827831042699)
XLA Ops:
  7.2 0.9 copy.57
  8.2 0.9 copy.60
  9.1 1.3 %reshape.49 = bf16[128,12,128]{2,1,0:T(8,128)(2,1)S(1)} reshape(bf16[2,8,8,1536]{3,2,1,0:T(8,128)(2,1)} %param.9) | data formatting | bytes 786432 | tf_op jit(solution)/shard_map/reshape | solution.py:108
  10.4 1.3 %reshape.50 = bf16[128,12,128]{2,1,0:T(8,128)(2,1)S(1)} reshape(bf16[2,8,8,1536]{3,2,1,0:T(8,128)(2,1)} %param.12) | data formatting | bytes 786432 | tf_op jit(solution)/shard_map/reshape | solution.py:109
  11.8 0.3 fusion.10
  12.1 0.2 convolution_bitcast_fusion.1
  12.3 0.3 fusion.11
  12.7 0.2 fusion.7
  12.9 0.8 pad_maximum_fusion.1
  13.8 0.5 collective-permute-start
  14.3 2.0 %collective-permute-start.1 = (bf16[2,2,2,8,1536]{4,3,2,1,0:T(8,128)(2,1)S(1)}, bf16[2,2,2,8,1536]{4,3,2,1,0:T(8,128)(2,1)S(1)}, u32[]{:S(2)}, u32[]{:S(2)}) collective-permute-start(bf16[2,2,2,8,1536]{4,3,2,1,0:T(8,128)(2,1)S(1)} %get-tuple-element.21), channel_id=1, source_target_pairs={{4,0},{8,4},{12,8},{0,12},{5,1},{9,5},{13,9},{1,13},{6,2},{10,6},{... | collective-permute-start | bytes 589832 | tf_op jit(solution)/shard_map/ppermute | solution.py:28
  16.3 0.7 convert_reduce_fusion
  17.0 0.1 convert_element_type.67
  17.1 2.5 %collective-permute-done = bf16[2,2,2,8,1536]{4,3,2,1,0:T(8,128)(2,1)S(1)} collective-permute-done((bf16[2,2,2,8,1536]{4,3,2,1,0:T(8,128)(2,1)S(1)}, bf16[2,2,2,8,1536]{4,3,2,1,0:T(8,128)(2,1)S(1)}, u32[]{:S(2)}, u32[]{:S(2)}) %collective-permute-start) | collective-permute-done | bytes 196640 | tf_op jit(solution)/shard_map/ppermute | solution.py:26
  19.6 1.9 %collective-permute-done.1 = bf16[2,2,2,8,1536]{4,3,2,1,0:T(8,128)(2,1)S(1)} collective-permute-done((bf16[2,2,2,8,1536]{4,3,2,1,0:T(8,128)(2,1)S(1)}, bf16[2,2,2,8,1536]{4,3,2,1,0:T(8,128)(2,1)S(1)}, u32[]{:S(2)}, u32[]{:S(2)}) %collective-permute-start.1) | collective-permute-done | bytes 196640 | tf_op jit(solution)/shard_map/ppermute | solution.py:28
  21.5 1.1 pad_maximum_fusion.5
  22.6 1.6 %collective-permute-start.2 = (bf16[2,2,12,2,1536]{4,3,2,1,0:T(2,128)(2,1)}, bf16[2,2,12,2,1536]{4,3,2,1,0:T(2,128)(2,1)S(1)}, u32[]{:S(2)}, u32[]{:S(2)}) collective-permute-start(bf16[2,2,12,2,1536]{4,3,2,1,0:T(2,128)(2,1)} %get-tuple-element.16), channel_id=1, source_target_pairs={{0,1},{1,2},{2,3},{3,0},{4,5},{5,6},{6,7},{7,4},{8,9},{9,10},{10,1... | collective-permute-start | bytes 884744 | tf_op jit(solution)/shard_map/ppermute | solution.py:26
  24.2 2.2 %collective-permute-start.3 = (bf16[2,2,12,2,1536]{4,3,2,1,0:T(2,128)(2,1)S(1)}, bf16[2,2,12,2,1536]{4,3,2,1,0:T(2,128)(2,1)S(1)}, u32[]{:S(2)}, u32[]{:S(2)}) collective-permute-start(bf16[2,2,12,2,1536]{4,3,2,1,0:T(2,128)(2,1)S(1)} %get-tuple-element.17), channel_id=1, source_target_pairs={{1,0},{2,1},{3,2},{0,3},{5,4},{6,5},{7,6},{4,7},{9,8},{10,9},{11,1... | collective-permute-start | bytes 884744 | tf_op jit(solution)/shard_map/ppermute | solution.py:28
  26.4 0.2 fusion.32
  26.6 0.2 fusion.31
  26.8 0.1 mul.62
  26.9 12.6 %collective-permute-done.2 = bf16[2,2,12,2,1536]{4,3,2,1,0:T(2,128)(2,1)S(1)} collective-permute-done((bf16[2,2,12,2,1536]{4,3,2,1,0:T(2,128)(2,1)}, bf16[2,2,12,2,1536]{4,3,2,1,0:T(2,128)(2,1)S(1)}, u32[]{:S(2)}, u32[]{:S(2)}) %collective-permute-start.2) | collective-permute-done | bytes 294944 | tf_op jit(solution)/shard_map/ppermute | solution.py:26
  39.6 12.6 %collective-permute-done.3 = bf16[2,2,12,2,1536]{4,3,2,1,0:T(2,128)(2,1)S(1)} collective-permute-done((bf16[2,2,12,2,1536]{4,3,2,1,0:T(2,128)(2,1)S(1)}, bf16[2,2,12,2,1536]{4,3,2,1,0:T(2,128)(2,1)S(1)}, u32[]{:S(2)}, u32[]{:S(2)}) %collective-permute-start.3) | collective-permute-done | bytes 294944 | tf_op jit(solution)/shard_map/ppermute | solution.py:28
  52.2 1.5 %pad_maximum_fusion = bf16[2,2,12,12,1536]{4,3,2,1,0:T(8,128)(2,1)S(1)} fusion(bf16[2,2,12,2,1536]{4,3,2,1,0:T(2,128)(2,1)S(1)} %collective-permute-done.3, bf16[2,2,2,8,1536]{4,3,2,1,0:T(8,128)(2,1)S(1)} %collective-permute-done.1, bf16[1,2,8,8,1536]{4,3,2,1,0:T(8,128)(2,1)S(1)} %bitcast.69, bf16[1,2,8,8,1536]{4,3,2,1,0:T(8,128)(2,1)S(1)} %bitcast.72, ...), kind=kLoop, calls=%fused_computation.2 | loop fusion | flops 10616832 | bytes 3538944 | tf_op jit(solution)/shard_map/concatenate | solution.py:24
  53.7 0.2 fusion.38
  53.9 1.6 %reshape_squeeze.9 = bf16[288,12,128]{2,1,0:T(8,128)(2,1)} reshape(bf16[1,2,12,12,1536]{4,3,2,1,0:T(8,128)(2,1)S(1)} %get-tuple-element.14) | data formatting | bytes 1769472 | tf_op jit(solution)/shard_map/reshape;squeeze | solution.py:113
  55.5 0.8 reshape_squeeze.8
  56.3 0.6 exponential_multiply_fusion
  56.9 1.1 copy-done.7
  58.0 0.5 multiply_convert_fusion
  58.5 0.4 multiply_bitcast_fusion
  58.9 0.3 copy-done.4
  59.2 0.3 copy-done.2
  59.6 2.5 %copy.73 = f32[288,12,128]{2,1,0:T(8,128)} copy(f32[288,12,128]{2,0,1:T(8,128)S(1)} %multiply_bitcast_fusion) | data formatting | bytes 3538944 | tf_op jit(solution)/shard_map/mul | solution.py:57
  62.1 2.4 %stack.30 = f32[1,2,12,12,1536]{4,3,2,1,0:T(8,128)S(1)} reshape(f32[288,12,128]{2,1,0:T(8,128)} %copy.73) | data formatting | bytes 3538944 | tf_op jit(solution)/shard_map/stack | solution.py:130
  64.5 1.9 %convolution_bitcast_fusion = f32[288,12,128]{2,0,1:T(8,128)S(1)} fusion(f32[12,288,128]{2,1,0:T(8,128)} %copy-done.4, bf16[128,12,128]{2,1,0:T(8,128)(2,1)S(1)} %reshape.50), kind=kOutput, calls=%fused_computation.9 | convolution fusion | flops 113688576 | bytes 3932160 | tf_op jit(solution)/shard_map/hqk,qhd->khd/dot_general | solution.py:45
  66.4 2.6 %copy.75 = f32[288,12,128]{2,1,0:T(8,128)} copy(f32[288,12,128]{2,0,1:T(8,128)S(1)} %convolution_bitcast_fusion) | data formatting | bytes 3538944 | tf_op jit(solution)/shard_map/hqk,qhd->khd/transpose | solution.py:45
  68.9 3.2 %stack.31 = f32[1,2,12,12,1536]{4,3,2,1,0:T(8,128)} reshape(f32[288,12,128]{2,1,0:T(8,128)} %copy.75) | data formatting | bytes 3538944 | tf_op jit(solution)/shard_map/stack | solution.py:130
  72.2 0.2 constant_dynamic-update-slice_fusion.1
  72.4 1.4 %copy-done.1 = f32[1,2,12,12,1536]{4,3,2,1,0:T(8,128)S(1)} copy-done((f32[1,2,12,12,1536]{4,3,2,1,0:T(8,128)S(1)}, f32[1,2,12,12,1536]{4,3,2,1,0:T(8,128)}, u32[]{:S(2)}) %copy-start.1) | copy-done | bytes 1769496
  73.8 0.2 constant_dynamic-update-slice_fusion
  74.1 0.1 fusion.36
  74.2 0.5 copy.78
  74.7 0.1 collective-permute-start.5
  74.7 0.5 copy.76
  75.2 0.5 collective-permute-start.4
  75.7 11.2 %collective-permute-done.5 = f32[2,2,2,12,1536]{4,2,3,1,0:T(2,128)S(1)} collective-permute-done((f32[2,2,2,12,1536]{4,2,3,1,0:T(2,128)S(1)}, f32[2,2,2,12,1536]{4,2,3,1,0:T(2,128)S(1)}, u32[]{:S(2)}, u32[]{:S(2)}) %collective-permute-start.5) | collective-permute-done | bytes 589856 | tf_op jit(solution)/shard_map/ppermute | solution.py:16
  86.9 0.1 copy.79
  87.1 3.4 %collective-permute-done.4 = f32[2,2,2,12,1536]{4,2,3,1,0:T(2,128)S(1)} collective-permute-done((f32[2,2,2,12,1536]{4,2,3,1,0:T(2,128)S(1)}, f32[2,2,2,12,1536]{4,2,3,1,0:T(2,128)S(1)}, u32[]{:S(2)}, u32[]{:S(2)}) %collective-permute-start.4) | collective-permute-done | bytes 589856 | tf_op jit(solution)/shard_map/ppermute | solution.py:16
  90.5 0.1 copy.77
  90.6 0.4 fusion
  91.1 1.2 fusion.37
  92.2 2.0 %collective-permute-start.6 = (f32[2,2,8,2,1536]{4,3,2,1,0:T(2,128)}, f32[2,2,8,2,1536]{4,3,2,1,0:T(2,128)}, u32[]{:S(2)}, u32[]{:S(2)}) collective-permute-start(f32[2,2,8,2,1536]{4,3,2,1,0:T(2,128)} %get-tuple-element.12), channel_id=1, source_target_pairs={{0,1},{1,2},{2,3},{3,0},{4,5},{5,6},{6,7},{7,4},{8,9},{9,10},{10,1... | collective-permute-start | bytes 1179656 | tf_op jit(solution)/shard_map/ppermute | solution.py:16
  94.2 1.9 %collective-permute-start.7 = (f32[2,2,8,2,1536]{4,3,2,1,0:T(2,128)}, f32[2,2,8,2,1536]{4,3,2,1,0:T(2,128)}, u32[]{:S(2)}, u32[]{:S(2)}) collective-permute-start(f32[2,2,8,2,1536]{4,3,2,1,0:T(2,128)} %get-tuple-element.13), channel_id=1, source_target_pairs={{0,3},{1,0},{2,1},{3,2},{4,7},{5,4},{6,5},{7,6},{8,11},{9,8},{10,9... | collective-permute-start | bytes 1179656 | tf_op jit(solution)/shard_map/ppermute | solution.py:16
  96.1 0.6 fusion.5
  96.7 1.1 fusion.6
  97.7 2.2 %copy.71 = bf16[128,12,128]{2,1,0:T(8,128)(2,1)} copy(bf16[128,12,128]{0,2,1:T(8,128)(2,1)} %fusion.6) | data formatting | bytes 786432 | tf_op jit(solution)/shard_map/convert_element_type | solution.py:127
  99.9 2.1 %reshape.53 = bf16[2,8,8,1536]{3,2,1,0:T(8,128)(2,1)} reshape(bf16[128,12,128]{2,1,0:T(8,128)(2,1)} %copy.71) | data formatting | bytes 786432 | tf_op jit(solution)/shard_map/reshape | solution.py:127
  102.0 4.4 %collective-permute-done.6 = f32[2,2,8,2,1536]{4,3,2,1,0:T(2,128)} collective-permute-done((f32[2,2,8,2,1536]{4,3,2,1,0:T(2,128)}, f32[2,2,8,2,1536]{4,3,2,1,0:T(2,128)}, u32[]{:S(2)}, u32[]{:S(2)}) %collective-permute-start.6) | collective-permute-done | bytes 393248 | tf_op jit(solution)/shard_map/ppermute | solution.py:16
  106.4 6.5 %collective-permute-done.7 = f32[2,2,8,2,1536]{4,3,2,1,0:T(2,128)} collective-permute-done((f32[2,2,8,2,1536]{4,3,2,1,0:T(2,128)}, f32[2,2,8,2,1536]{4,3,2,1,0:T(2,128)}, u32[]{:S(2)}, u32[]{:S(2)}) %collective-permute-start.7) | collective-permute-done | bytes 393248 | tf_op jit(solution)/shard_map/ppermute | solution.py:16
  112.9 1.6 %fusion.2 = bf16[2,2,8,8,1536]{4,3,2,1,0:T(8,128)(2,1)S(1)} fusion(f32[2,2,8,12,1536]{4,3,2,1,0:T(8,128)S(1)} %fusion, f32[2,2,8,2,1536]{4,3,2,1,0:T(2,128)} %collective-permute-done.7, f32[2,2,8,2,1536]{4,3,2,1,0:T(2,128)} %collective-permute-done.6), kind=kLoop, calls=%fused_computation.8 | loop fusion | flops 1179648 | bytes 3145728 | tf_op jit(solution)/shard_map/convert.3
  114.5 0.9 slice_bitcast_fusion
  115.4 3.5 %reduce_sum.9 = bf16[2,32,12,128]{3,1,2,0:T(8,128)(2,1)S(1)} reduce(f32[16,2,32,12,128]{4,2,3,1,0:T(8,128)} %bitcast.66, f32[]{:T(128)} %constant.7.clone.1), dimensions={0}, to_apply=%region_0.0 | reduce | flops 1474560 | bytes 6488068 | tf_op jit(solution)/shard_map/reduce_sum | solution.py:129
  119.0 0.7 copy_bitcast_fusion
  (31 shorter events, 0.3 us)
Async XLA Ops:
  7.2 4.6 %copy-start = (bf16[32,1536]{1,0:T(8,128)(2,1)S(1)}, bf16[32,1536]{1,0:T(8,128)(2,1)}, u32[]{:S(2)}) copy-start(bf16[32,1536]{1,0:T(8,128)(2,1)} %param.15) | copy-start | bytes 294916
  7.2 5.2 %copy-start.12 = (bf16[32,1536]{1,0:T(8,128)(2,1)S(1)}, bf16[32,1536]{1,0:T(8,128)(2,1)}, u32[]{:S(2)}) copy-start(bf16[32,1536]{1,0:T(8,128)(2,1)} %param.16) | copy-start | bytes 294916
  7.2 108.2 %all-gather.3.cloned.1.call-start = ((), (), s32[]{:S(2)}) async-start(), calls=%async_computation | async-start | bytes 6684672 | tf_op jit(solution)/shard_map/all_gather | solution.py:129
  10.4 3.3 %copy-start.8 = (bf16[2,8,8,1536]{3,2,1,0:T(8,128)(2,1)S(1)}, bf16[2,8,8,1536]{3,2,1,0:T(8,128)(2,1)}, u32[]{:S(2)}) copy-start(bf16[2,8,8,1536]{3,2,1,0:T(8,128)(2,1)} %param.11) | copy-start | bytes 1179652
  10.4 3.3 %copy-start.9 = (bf16[2,8,8,1536]{3,2,1,0:T(8,128)(2,1)S(1)}, bf16[2,8,8,1536]{3,2,1,0:T(8,128)(2,1)}, u32[]{:S(2)}) copy-start(bf16[2,8,8,1536]{3,2,1,0:T(8,128)(2,1)} %param.10) | copy-start | bytes 1179652
  12.7 9.9 %copy-start.10 = (bf16[12,128,32]{1,2,0:T(8,128)(2,1)}, bf16[12,128,32]{1,2,0:T(8,128)(2,1)S(1)}, u32[]{:S(2)}) copy-start(bf16[12,128,32]{1,2,0:T(8,128)(2,1)S(1)} %fusion.11) | copy-start | bytes 294916
  13.8 5.8 %collective-permute-start = (bf16[2,2,2,8,1536]{4,3,2,1,0:T(8,128)(2,1)S(1)}, bf16[2,2,2,8,1536]{4,3,2,1,0:T(8,128)(2,1)S(1)}, u32[]{:S(2)}, u32[]{:S(2)}) collective-permute-start(bf16[2,2,2,8,1536]{4,3,2,1,0:T(8,128)(2,1)S(1)} %get-tuple-element.20), channel_id=1, source_target_pairs={{0,4},{4,8},{8,12},{12,0},{1,5},{5,9},{9,13},{13,1},{2,6},{6,10},{... | collective-permute-start | bytes 589832 | tf_op jit(solution)/shard_map/ppermute | solution.py:26
  14.3 7.2 %collective-permute-start.1 = (bf16[2,2,2,8,1536]{4,3,2,1,0:T(8,128)(2,1)S(1)}, bf16[2,2,2,8,1536]{4,3,2,1,0:T(8,128)(2,1)S(1)}, u32[]{:S(2)}, u32[]{:S(2)}) collective-permute-start(bf16[2,2,2,8,1536]{4,3,2,1,0:T(8,128)(2,1)S(1)} %get-tuple-element.21), channel_id=1, source_target_pairs={{4,0},{8,4},{12,8},{0,12},{5,1},{9,5},{13,9},{1,13},{6,2},{10,6},{... | collective-permute-start | bytes 589832 | tf_op jit(solution)/shard_map/ppermute | solution.py:28
  22.6 17.0 %collective-permute-start.2 = (bf16[2,2,12,2,1536]{4,3,2,1,0:T(2,128)(2,1)}, bf16[2,2,12,2,1536]{4,3,2,1,0:T(2,128)(2,1)S(1)}, u32[]{:S(2)}, u32[]{:S(2)}) collective-permute-start(bf16[2,2,12,2,1536]{4,3,2,1,0:T(2,128)(2,1)} %get-tuple-element.16), channel_id=1, source_target_pairs={{0,1},{1,2},{2,3},{3,0},{4,5},{5,6},{6,7},{7,4},{8,9},{9,10},{10,1... | collective-permute-start | bytes 884744 | tf_op jit(solution)/shard_map/ppermute | solution.py:26
  24.2 28.0 %collective-permute-start.3 = (bf16[2,2,12,2,1536]{4,3,2,1,0:T(2,128)(2,1)S(1)}, bf16[2,2,12,2,1536]{4,3,2,1,0:T(2,128)(2,1)S(1)}, u32[]{:S(2)}, u32[]{:S(2)}) collective-permute-start(bf16[2,2,12,2,1536]{4,3,2,1,0:T(2,128)(2,1)S(1)} %get-tuple-element.17), channel_id=1, source_target_pairs={{1,0},{2,1},{3,2},{0,3},{5,4},{6,5},{7,6},{4,7},{9,8},{10,9},{11,1... | collective-permute-start | bytes 884744 | tf_op jit(solution)/shard_map/ppermute | solution.py:28
  56.3 2.2 %copy-start.5 = (bf16[288,12,128]{2,1,0:T(8,128)(2,1)}, bf16[288,12,128]{2,1,0:T(8,128)(2,1)S(1)}, u32[]{:S(2)}) copy-start(bf16[288,12,128]{2,1,0:T(8,128)(2,1)S(1)} %reshape_squeeze.8) | copy-start | bytes 2654212
  56.3 1.7 %copy-start.7 = (bf16[288,12,128]{2,1,0:T(8,128)(2,1)S(1)}, bf16[288,12,128]{2,1,0:T(8,128)(2,1)}, u32[]{:S(2)}) copy-start(bf16[288,12,128]{2,1,0:T(8,128)(2,1)} %reshape_squeeze.9) | copy-start | bytes 2654212
  58.0 1.2 copy-start.4
  58.5 1.1 copy-start.2
  72.2 1.7 %copy-start.1 = (f32[1,2,12,12,1536]{4,3,2,1,0:T(8,128)S(1)}, f32[1,2,12,12,1536]{4,3,2,1,0:T(8,128)}, u32[]{:S(2)}) copy-start(f32[1,2,12,12,1536]{4,3,2,1,0:T(8,128)} %stack.31) | copy-start | bytes 5308420
  74.7 12.3 %collective-permute-start.5 = (f32[2,2,2,12,1536]{4,2,3,1,0:T(2,128)S(1)}, f32[2,2,2,12,1536]{4,2,3,1,0:T(2,128)S(1)}, u32[]{:S(2)}, u32[]{:S(2)}) collective-permute-start(f32[2,2,2,12,1536]{4,2,3,1,0:T(2,128)S(1)} %copy.78), channel_id=1, source_target_pairs={{0,12},{4,0},{8,4},{12,8},{1,13},{5,1},{9,5},{13,9},{2,14},{6,2},{... | collective-permute-start | bytes 1769480 | tf_op jit(solution)/shard_map/ppermute | solution.py:16
  75.2 15.3 %collective-permute-start.4 = (f32[2,2,2,12,1536]{4,2,3,1,0:T(2,128)S(1)}, f32[2,2,2,12,1536]{4,2,3,1,0:T(2,128)S(1)}, u32[]{:S(2)}, u32[]{:S(2)}) collective-permute-start(f32[2,2,2,12,1536]{4,2,3,1,0:T(2,128)S(1)} %copy.76), channel_id=1, source_target_pairs={{0,4},{4,8},{8,12},{12,0},{1,5},{5,9},{9,13},{13,1},{2,6},{6,10},{... | collective-permute-start | bytes 1769480 | tf_op jit(solution)/shard_map/ppermute | solution.py:16
  90.6 5.5 %copy-start.3 = (bf16[12,288,128]{2,1,0:T(8,128)(2,1)S(1)}, bf16[12,288,128]{2,1,0:T(8,128)(2,1)}, u32[]{:S(2)}) copy-start(bf16[12,288,128]{2,1,0:T(8,128)(2,1)} %copy-done.2) | copy-start | bytes 2654212
  90.6 5.4 %copy-start.6 = (bf16[288,12,128]{2,1,0:T(8,128)(2,1)S(1)}, bf16[288,12,128]{2,1,0:T(8,128)(2,1)}, u32[]{:S(2)}) copy-start(bf16[288,12,128]{2,1,0:T(8,128)(2,1)} %copy-done.5) | copy-start | bytes 2654212
  91.0 5.6 %copy-start.11 = (bf16[12,128,32]{1,2,0:T(8,128)(2,1)S(1)}, bf16[12,128,32]{1,2,0:T(8,128)(2,1)}, u32[]{:S(2)}) copy-start(bf16[12,128,32]{1,2,0:T(8,128)(2,1)} %copy-done.10) | copy-start | bytes 294916
  92.2 14.1 %collective-permute-start.6 = (f32[2,2,8,2,1536]{4,3,2,1,0:T(2,128)}, f32[2,2,8,2,1536]{4,3,2,1,0:T(2,128)}, u32[]{:S(2)}, u32[]{:S(2)}) collective-permute-start(f32[2,2,8,2,1536]{4,3,2,1,0:T(2,128)} %get-tuple-element.12), channel_id=1, source_target_pairs={{0,1},{1,2},{2,3},{3,0},{4,5},{5,6},{6,7},{7,4},{8,9},{9,10},{10,1... | collective-permute-start | bytes 1179656 | tf_op jit(solution)/shard_map/ppermute | solution.py:16
  94.2 18.7 %collective-permute-start.7 = (f32[2,2,8,2,1536]{4,3,2,1,0:T(2,128)}, f32[2,2,8,2,1536]{4,3,2,1,0:T(2,128)}, u32[]{:S(2)}, u32[]{:S(2)}) collective-permute-start(f32[2,2,8,2,1536]{4,3,2,1,0:T(2,128)} %get-tuple-element.13), channel_id=1, source_target_pairs={{0,3},{1,0},{2,1},{3,2},{4,7},{5,4},{6,5},{7,6},{8,11},{9,8},{10,9... | collective-permute-start | bytes 1179656 | tf_op jit(solution)/shard_map/ppermute | solution.py:16
Sparse Core Ops, SparseCore 0:
  13.8 76.6 all-gather.2
